TPU v7x, 32 devices: a whole 2x2x4 slice. The times are simulated.
32 devices in a mesh: rep: 2 (over y), own: 16 (over z, x, core).
Axes of the slice: x: 2, y: 2, z: 4, core: 2. Of those that a mesh axis runs over, the one named last changes fastest.
Arguments:
- values: float32 [262144, 128], P(('rep', 'own')), may hold values from -0.8 to 0.8
- key_ids: int32 [262144], P(('rep', 'own')), may hold values from 0 to 65535, as said below
- heavy_ids: int32 [2048], replicated, may hold values from 0 to 65535, as said below
- block_offsets: int32 [32, 16], P(('rep', 'own')), may hold values from 0 to 8191, as said below
- block_counts: int32 [32, 16], P(('rep', 'own')), may hold values from 8 to 64, as said below
Outputs:
- light_sums: float32 [65536, 128], P('own')
- heavy_sums: float32 [2048, 128], P('own')
Inputs may be any that keep to these rules, and one draw needn't show every extreme that they name: `key_ids`: an event in block o of a device has a key in o * 4096 to (o + 1) * 4096 - 1 that is not a heavy key; every event outside all blocks has a heavy key. `heavy_ids`: distinct keys. `block_offsets`: on each device the blocks lie in the order of o, do not meet, and end by position 8192. `block_counts`: at most 64; one owner gets exactly 64 from every device.
All inputs are finite; a program needn't handle non-finite values.
Results may differ from a plain program's by a relative error of at most 0.000075.
Values sent between devices are 32-bit elements; how exact they have to be, the bound alone decides.
A program may use at most 64 MiB of HBM per device.

v0:
```python
import math

import jax
import jax.numpy as jnp
from jax import lax
from jax.sharding import PartitionSpec as P

KEYS_DEV = 4096
CAP = 64


def key_sums(rows_in, row_keys, targets):
    slots = row_keys.shape[0]
    block_len = math.gcd(slots, 2048)
    count_blocks = slots // block_len
    rows_blocks = rows_in.reshape(count_blocks, block_len, rows_in.shape[1])
    keys_blocks = row_keys.reshape(count_blocks, block_len)

    def accumulate(running, pieces):
        rows_piece, keys_piece = pieces
        onehot = (targets[:, None] == keys_piece[None, :]).astype(jnp.float32)
        added = jnp.dot(
            onehot, rows_piece, precision=lax.Precision.HIGHEST, preferred_element_type=jnp.float32
        )
        return (running + added, None)

    start_sums = jnp.zeros((targets.shape[0], rows_in.shape[1]), jnp.float32)
    running, unused = lax.scan(accumulate, start_sums, (rows_blocks, keys_blocks))
    return running


def per_device(values, key_ids, heavy_ids, block_offsets, block_counts):
    owners = lax.axis_size("own")
    pairs = lax.axis_size("rep")
    own_index = lax.axis_index("own")
    rep_index = lax.axis_index("rep")
    width = values.shape[1]
    slot_cap = CAP
    padded_values = jnp.concatenate([values, jnp.zeros((slot_cap, width), jnp.float32)], axis=0)
    padded_keys = jnp.concatenate([key_ids, jnp.full((slot_cap,), -1, jnp.int32)], axis=0)
    slot_iota = jnp.arange(slot_cap, dtype=jnp.int32)
    positions = block_offsets[0][:, None] + slot_iota[None, :]
    valid = slot_iota[None, :] < block_counts[0][:, None]
    block_rows = jnp.where(valid[:, :, None], jnp.take(padded_values, positions, axis=0), 0.0)
    block_keys = jnp.where(valid, jnp.take(padded_keys, positions, axis=0), -1)
    half_keys = KEYS_DEV // 2
    owner_base = (jnp.arange(owners, dtype=jnp.int32) * KEYS_DEV)[:, None]
    which_half = jnp.where(block_keys >= 0, (block_keys - owner_base) // half_keys, -1)
    split_rows = jnp.stack(
        [jnp.where((which_half == side)[:, :, None], block_rows, 0.0) for side in range(pairs)],
        axis=0,
    )
    split_keys = jnp.stack(
        [jnp.where(which_half == side, block_keys, -1) for side in range(pairs)], axis=0
    )
    split_rows = split_rows.reshape(pairs * owners, slot_cap, width)
    split_keys = split_keys.reshape(pairs * owners, slot_cap)
    got_rows, got_keys = (
        lax.all_to_all(split_rows, ("rep", "own"), split_axis=0, concat_axis=0, tiled=True),
        lax.all_to_all(split_keys, ("rep", "own"), split_axis=0, concat_axis=0, tiled=True),
    )
    local_keys = jnp.where(
        got_keys >= 0, got_keys - own_index * KEYS_DEV - rep_index * half_keys, -1
    ).reshape(-1)
    owned_half = key_sums(
        got_rows.reshape(-1, width), local_keys, jnp.arange(half_keys, dtype=jnp.int32)
    )
    light_sums = lax.all_gather(owned_half, "rep", axis=0, tiled=True)
    partial_sums = key_sums(values, key_ids, heavy_ids)
    summed_pair = lax.psum(partial_sums, "rep")
    heavy_sums = lax.psum_scatter(summed_pair, "own", scatter_dimension=0, tiled=True)
    return (light_sums, heavy_sums)


def solution(mesh):
    placed = (
        P(("rep", "own"), None),
        P(("rep", "own")),
        P(),
        P(("rep", "own"), None),
        P(("rep", "own"), None),
    )
    return jax.shard_map(
        per_device,
        mesh=mesh,
        in_specs=placed,
        out_specs=(P("own", None), P("own", None)),
        check_vma=False,
    )
```

profile of v0, /device:TPU:0, one launch (start us, length us, event | category | flops | bytes accessed | tf_op | source)
XLA Modules:
  0.0 166.0 jit_solution(6468750620577032743)
XLA Ops:
  8.0 0.7 compare_select_fusion.2
  8.7 0.1 reshape.548
  8.8 0.8 concatenate.6
  9.6 0.0 copy-start.3
  9.6 0.0 copy-start.4
  9.6 6.1 %gather_fusion = s32[1024]{0:T(1024)S(1)} fusion(s32[8256]{0:T(1024)S(1)} %concatenate.6, s32[1024]{0:T(1024)S(1)} %broadcast_clamp_fusion), kind=kCustom, calls=%fused_computation | custom fusion | bytes 12288 | tf_op jit(solution)/shard_map/jit(_take)/gather | solution.py:45
  15.7 0.1 gather.13
  15.8 0.0 copy-done.3
  15.8 0.0 copy-done.4
  15.8 0.1 compare_select_fusion.5
  15.9 0.6 pad_add_fusion
  16.5 7.3 %all-to-all-start = ((s32[32,1,64]{2,1,0:T(1,128)}), s32[32,1,64]{2,1,0:T(1,128)S(1)}, u32[]{:S(2)}, u32[]{:S(2)}) async-start(s32[32,1,64]{2,1,0:T(1,128)} %bitcast.2), calls=%async_computation | async-start | bytes 32768 | tf_op jit(solution)/shard_map/all_to_all | solution.py:60
  23.8 0.1 reshape.547
  23.9 3.7 %concatenate.7 = f32[8256,128]{1,0:T(8,128)} pad(f32[8192,128]{1,0:T(8,128)} %param.7, f32[]{:T(128)} %constant.82.clone.1), padding=0_64x0_0 | pad | bytes 8421380 | tf_op jit(solution)/shard_map/concatenate | solution.py:39
  27.6 0.0 copy-start.1
  27.6 0.0 copy-start.5
  27.6 5.0 %gather_fusion.1 = f32[1024,128]{1,0:T(8,128)S(1)} fusion(f32[8256,128]{1,0:T(8,128)} %concatenate.7, s32[1024]{0:T(1024)S(1)} %broadcast_clamp_fusion), kind=kCustom, calls=%fused_computation.1 | custom fusion | bytes 1052672 | tf_op jit(solution)/shard_map/jit(_take)/gather | solution.py:44
  32.6 0.1 broadcast_compare_fusion.1
  32.8 0.7 fusion.13
  33.5 1.1 pad_maximum_fusion
  34.6 0.0 copy-done.1
  34.6 0.0 all-to-all-done
  34.6 5.8 %all-to-all-start.1 = ((f32[32,64,128]{2,1,0:T(8,128)}), f32[32,64,128]{2,1,0:T(8,128)S(1)}, u32[]{:S(2)}, u32[]{:S(2)}) async-start(f32[32,64,128]{2,1,0:T(8,128)} %bitcast.4), calls=%async_computation.1 | async-start | bytes 2097152 | tf_op jit(solution)/shard_map/all_to_all | solution.py:59
  40.4 0.0 reduce-scatter.2.cloned.1.call-start
  40.5 0.0 copy-done.5
  40.5 34.5 %while.3 = (s32[]{:T(128)}, f32[2048,128]{1,0:T(8,128)S(1)}, s32[2048]{0:T(1024)S(1)}, s32[4,2048]{1,0:T(4,128)S(1)}, f32[4,2048,128]{2,1,0:T(8,128)}, /*index=5*/s32[]{:T(128)}, s32[]{:T(128)}) while((s32[]{:T(128)}, f32[2048,128]{1,0:T(8,128)S(1)}, s32[2048]{0:T(1024)S(1)}, s32[4,2048]{1,0:T(4,128)S(1)}, ...), condition=%wide.region_1.2_spmd.clone, body=%wide.region_0.1_spmd.clone.sunk | while | flops 6447169536 | bytes 3178599 | solution.py:28
  40.5 8.6 %fusion.34 = f32[2048,128]{1,0:T(8,128)S(1)} fusion(s32[2048]{0:T(1024)S(1)} %bitcast.21, s32[2048]{0:T(1024)S(1)} %get-tuple-element.128, f32[2048,128]{1,0:T(8,128)S(1)} %get-tuple-element.120, f32[4,2048,128]{2,1,0:T(8,128)} %get-tuple-element.130, s32[]{:T(128)S(6)} %copy.9, pred[]{:T(512)S(6)} %compare.29), kind=kOutput, calls=%fused_computation.6.clone.1 | convolution fusion | flops 6447169536 | bytes 3162117 | tf_op jit(solution)/shard_map/while/body/eval_jaxpr/dot_general | solution.py:22
  49.2 8.6 %fusion.34 = f32[2048,128]{1,0:T(8,128)S(1)} fusion(s32[2048]{0:T(1024)S(1)} %bitcast.21, s32[2048]{0:T(1024)S(1)} %get-tuple-element.128, f32[2048,128]{1,0:T(8,128)S(1)} %get-tuple-element.120, f32[4,2048,128]{2,1,0:T(8,128)} %get-tuple-element.130, s32[]{:T(128)S(6)} %copy.9, pred[]{:T(512)S(6)} %compare.29), kind=kOutput, calls=%fused_computation.6.clone.1 | convolution fusion | flops 6447169536 | bytes 3162117 | tf_op jit(solution)/shard_map/while/body/eval_jaxpr/dot_general | solution.py:22
  57.8 8.6 %fusion.34 = f32[2048,128]{1,0:T(8,128)S(1)} fusion(s32[2048]{0:T(1024)S(1)} %bitcast.21, s32[2048]{0:T(1024)S(1)} %get-tuple-element.128, f32[2048,128]{1,0:T(8,128)S(1)} %get-tuple-element.120, f32[4,2048,128]{2,1,0:T(8,128)} %get-tuple-element.130, s32[]{:T(128)S(6)} %copy.9, pred[]{:T(512)S(6)} %compare.29), kind=kOutput, calls=%fused_computation.6.clone.1 | convolution fusion | flops 6447169536 | bytes 3162117 | tf_op jit(solution)/shard_map/while/body/eval_jaxpr/dot_general | solution.py:22
  66.4 8.6 %fusion.34 = f32[2048,128]{1,0:T(8,128)S(1)} fusion(s32[2048]{0:T(1024)S(1)} %bitcast.21, s32[2048]{0:T(1024)S(1)} %get-tuple-element.128, f32[2048,128]{1,0:T(8,128)S(1)} %get-tuple-element.120, f32[4,2048,128]{2,1,0:T(8,128)} %get-tuple-element.130, s32[]{:T(128)S(6)} %copy.9, pred[]{:T(512)S(6)} %compare.29), kind=kOutput, calls=%fused_computation.6.clone.1 | convolution fusion | flops 6447169536 | bytes 3162117 | tf_op jit(solution)/shard_map/while/body/eval_jaxpr/dot_general | solution.py:22
  75.0 0.0 copy-start
  75.0 1.0 copy-done
  76.0 0.0 reduce-scatter.2.cloned.1.call-update
  76.0 0.2 all-gather.2.cloned.1.call-start
  76.2 0.1 fusion.14
  76.3 0.1 select_n.222
  76.4 0.0 all-to-all-done.1
  76.4 8.6 %fusion.10 = f32[2048,128]{1,0:T(8,128)} fusion(f32[2048,128]{1,0:T(8,128)S(1)} %bitcast.20, s32[2048]{0:T(1024)S(1)} %select_n.222), kind=kOutput, calls=%fused_computation.12 | convolution fusion | flops 6446645248 | bytes 2105344 | tf_op jit(solution)/shard_map/while/body/eval_jaxpr/dot_general | solution.py:22
  84.9 0.0 all-gather.2.cloned.1.call-update
  85.0 0.0 all-reduce.4.cloned.1.call-start
  85.0 49.9 %reduce-scatter.2.cloned.1.call-done = f32[128,128]{1,0:T(8,128)} async-done(((f32[2048,128]{1,0:T(8,128)}), f32[128,128]{1,0:T(8,128)}) %reduce-scatter.2.cloned.1.call-update) | async-done | bytes 65552 | tf_op jit(solution)/shard_map/reduce_scatter | solution.py:71
  134.9 0.0 all-reduce.4.cloned.1.call-update
  135.0 0.0 all-gather.2.cloned.1.call-done
  135.0 19.8 %all-reduce.4.cloned.1.call-done = f32[128,128]{1,0:T(8,128)} async-done(((f32[128,128]{1,0:T(8,128)}), f32[128,128]{1,0:T(8,128)}) %all-reduce.4.cloned.1.call-update) | async-done | bytes 65552 | tf_op jit(solution)/shard_map/psum | solution.py:70
  154.8 0.0 copy-start.2
  154.8 3.1 %copy.15 = f32[4096,128]{1,0:T(8,128)} copy(f32[4096,128]{1,0:T(8,128)} %all-gather.2.cloned.1.call-done) | data formatting | bytes 4194304
  157.9 0.0 copy-done.2
  157.9 0.6 copy.16
  (9 shorter events, 0.1 us)
Async XLA Ops:
  9.6 6.2 %copy-start.3 = (s32[1,16]{1,0:T(1,128)S(1)}, s32[1,16]{1,0:T(1,128)}, u32[]{:S(2)}) copy-start(s32[1,16]{1,0:T(1,128)} %param.10) | copy-start | bytes 196
  9.6 6.2 %copy-start.4 = (s32[1,16]{1,0:T(1,128)S(1)}, s32[1,16]{1,0:T(1,128)}, u32[]{:S(2)}) copy-start(s32[1,16]{1,0:T(1,128)} %param.11) | copy-start | bytes 196
  16.5 18.1 %all-to-all-start = ((s32[32,1,64]{2,1,0:T(1,128)}), s32[32,1,64]{2,1,0:T(1,128)S(1)}, u32[]{:S(2)}, u32[]{:S(2)}) async-start(s32[32,1,64]{2,1,0:T(1,128)} %bitcast.2), calls=%async_computation | async-start | bytes 32768 | tf_op jit(solution)/shard_map/all_to_all | solution.py:60
  27.6 6.9 %copy-start.1 = (s32[8192]{0:T(1024)S(1)}, s32[8192]{0:T(1024)}, u32[]{:S(2)}) copy-start(s32[8192]{0:T(1024)} %param.8) | copy-start | bytes 98308
  27.6 12.9 %copy-start.5 = (s32[2048]{0:T(1024)S(1)}, s32[2048]{0:T(1024)}, u32[]{:S(2)}) copy-start(s32[2048]{0:T(1024)} %param.9) | copy-start | bytes 24580
  34.6 41.8 %all-to-all-start.1 = ((f32[32,64,128]{2,1,0:T(8,128)}), f32[32,64,128]{2,1,0:T(8,128)S(1)}, u32[]{:S(2)}, u32[]{:S(2)}) async-start(f32[32,64,128]{2,1,0:T(8,128)} %bitcast.4), calls=%async_computation.1 | async-start | bytes 2097152 | tf_op jit(solution)/shard_map/all_to_all | solution.py:59
  40.4 94.5 %reduce-scatter.2.cloned.1.call-start = ((), (), s32[]{:S(2)}) async-start(), calls=%async_computation.4 | async-start | bytes 1114112 | tf_op jit(solution)/shard_map/reduce_scatter | solution.py:71
  75.0 1.0 copy-start
  76.0 59.0 %all-gather.2.cloned.1.call-start = ((), (), s32[]{:S(2)}) async-start(), calls=%async_computation.3 | async-start | bytes 3145728 | tf_op jit(solution)/shard_map/all_gather | solution.py:68
  85.0 69.9 %all-reduce.4.cloned.1.call-start = ((), (), s32[]{:S(2)}) async-start(), calls=%async_computation.5 | async-start | bytes 131072 | tf_op jit(solution)/shard_map/psum | solution.py:70
  154.8 3.1 %copy-start.2 = (f32[128,128]{1,0:T(8,128)S(1)}, f32[128,128]{1,0:T(8,128)}, u32[]{:S(2)}) copy-start(f32[128,128]{1,0:T(8,128)} %all-reduce.4.cloned.1.call-done) | copy-start | bytes 196612
Sparse Core Ops, SparseCore 0:
  76.1 58.7 reduce-scatter.1
Sparse Core Ops, SparseCore 1:
  85.0 34.2 all-gather.1
  135.0 19.7 all-reduce.3
where the time goes:
time: 166 us
  waiting for transfers between devices  69.8 us (42%)
  matrix products  42.9 us (26%)
  local copies, waits for them, and re-layouts  20.6 us (12%)
  between operations  15.6 us (9%)
  starting transfers between devices  13.5 us (8%)
  other arithmetic  3.39 us (2%)
    reduce_scatter x1, waiting for transfers between devices, per_device(): lax.psum_scatter(summed_pair, 'own', scatter_dimension=0, tiled=True)  49.9 us
    dot_general x5, matrix products, accumulate(): jnp.dot(onehot, rows_piece, precision=lax.Precision.HIGHEST, preferred_el...  42.9 us
    psum x1, waiting for transfers between devices, per_device(): summed_pair = lax.psum(partial_sums, 'rep')  19.8 us
    all_to_all x1, starting transfers between devices, per_device(): lax.all_to_all(split_keys, ('rep', 'own'), split_axis=0, concat_axis=0, t...  7.33 us
    gather x3, local copies, waits for them, and re-layouts, per_device(): block_keys = jnp.where(valid, jnp.take(padded_keys, positions, axis=0), -1)  6.28 us
    all_to_all x1, starting transfers between devices, per_device(): lax.all_to_all(split_rows, ('rep', 'own'), split_axis=0, concat_axis=0, t...  5.84 us
    gather x1, local copies, waits for them, and re-layouts, per_device(): jnp.take(padded_values, positions, axis=0)  5 us
    unnamed x14, local copies, waits for them, and re-layouts  4.68 us
  transfers between devices with their start and end apart: 5, of which 2 were waited for; matrix products, arithmetic and copies ran while one was open for 32% of the time, Pallas kernels for 0%

commit v1 on v0

v1 whole, which is shorter than its diff:
```python
import functools
import math

import jax
import jax.numpy as jnp
from jax import lax
from jax.experimental import pallas as pl
from jax.experimental.pallas import tpu as pltpu
from jax.sharding import PartitionSpec as P

CAP = 64
LANES = 128


def split_bf16(rows):
    high = rows.astype(jnp.bfloat16)
    low = (rows - high.astype(jnp.float32)).astype(jnp.bfloat16)
    return jnp.concatenate([high, low], axis=1)


def pack_kernel(owners, events, offs, cnts, vals, keys, out, stage, sems):
    def start_of(o):
        return jnp.minimum(offs[0, o], events - CAP)

    def copy_of(o):
        base = pl.multiple_of(jnp.minimum((start_of(o) // 8) * 8, events - CAP - 8), 8)
        return base, pltpu.make_async_copy(
            vals.at[pl.ds(base, CAP + 8)], stage.at[o], sems.at[o]
        )

    @pl.loop(0, owners)
    def _(o):
        copy_of(o)[1].start()

    lane = lax.broadcasted_iota(jnp.int32, (1, LANES), 1)
    last_row = events // LANES - 1

    @pl.loop(0, owners)
    def _(o):
        base, copy = copy_of(o)
        copy.wait()
        start = start_of(o)
        skip = offs[0, o] - start
        out[o, 0:CAP, :] = stage[o, pl.ds(start - base, CAP), :]
        row = start // LANES
        shift = start % LANES
        back = (LANES - shift) % LANES
        first = pltpu.roll(keys[pl.ds(row, 1), :], back, 1)
        second = pltpu.roll(keys[pl.ds(jnp.minimum(row + 1, last_row), 1), :], back, 1)
        joined = jnp.where(lane < LANES - shift, first, second)
        valid = (lane >= skip) & (lane < skip + cnts[0, o]) & (lane < CAP)
        block = jnp.where(valid, joined, -1)
        twice = jnp.where(lane < CAP, block, pltpu.roll(block, CAP, 1))
        out[o, CAP : CAP + 8, :] = jnp.broadcast_to(twice, (8, LANES)).astype(jnp.float32)


def pack(values, keys2d, offsets, counts, owners):
    events, width = values.shape
    smem = pl.BlockSpec(memory_space=pltpu.SMEM)
    vmem = pl.BlockSpec(memory_space=pltpu.VMEM)
    return pl.pallas_call(
        functools.partial(pack_kernel, owners, events),
        out_shape=jax.ShapeDtypeStruct((owners, CAP + 8, width), jnp.float32),
        in_specs=[smem, smem, pl.BlockSpec(memory_space=pl.ANY), vmem],
        out_specs=vmem,
        scratch_shapes=[
            pltpu.VMEM((owners, CAP + 8, width), jnp.float32),
            pltpu.SemaphoreType.DMA((owners,)),
        ],
        name="pack",
    )(offsets, counts, values, keys2d)


def heavy_kernel(step_k, pairs, rows_owner, vals, keys, heavy, out, rhs):
    events = vals.shape[0]
    steps = events // step_k
    chunk = heavy.shape[0]
    half = rows_owner // pairs

    @pl.when(pl.program_id(0) == 0)
    def _():
        @pl.loop(0, steps)
        def _(s):
            at = pl.ds(pl.multiple_of(s * step_k, step_k), step_k)
            rhs[at, :] = split_bf16(vals[at, :])

    targets = heavy[...]
    acc = jnp.zeros((chunk, rhs.shape[1]), jnp.float32)

    def body(s, acc):
        at = pl.ds(pl.multiple_of(s * step_k, step_k), step_k)
        pieces = []
        for c in range(step_k // LANES):
            row = keys[pl.ds(s * (step_k // LANES) + c, 1), :]
            pieces.append(jnp.where(targets == row, 1.0, 0.0).astype(jnp.bfloat16))
        onehot = jnp.concatenate(pieces, axis=1)
        return acc + jnp.dot(onehot, rhs[at, :], preferred_element_type=jnp.float32)

    acc = lax.fori_loop(0, steps, body, acc)
    width = vals.shape[1]
    sums = acc[:, :width] + acc[:, width:]
    for o in range(chunk // rows_owner):
        for r in range(pairs):
            begin = o * rows_owner + r * half
            out[r, o] = sums[begin : begin + half]


def heavy_partials(values, keys2d, heavy_wide, pairs, owners):
    events, width = values.shape
    heavy = heavy_wide.shape[0]
    rows_owner = heavy // owners
    chunk = max(rows_owner, min(256, heavy))
    per = chunk // rows_owner
    half = rows_owner // pairs
    return pl.pallas_call(
        functools.partial(heavy_kernel, 1024, pairs, rows_owner),
        out_shape=jax.ShapeDtypeStruct((pairs, owners, half, width), jnp.float32),
        grid=(heavy // chunk,),
        in_specs=[
            pl.BlockSpec((events, width), lambda i: (0, 0), pipeline_mode=pl.Buffered(1)),
            pl.BlockSpec(keys2d.shape, lambda i: (0, 0), pipeline_mode=pl.Buffered(1)),
            pl.BlockSpec((chunk, LANES), lambda i: (i, 0)),
        ],
        out_specs=pl.BlockSpec((pairs, per, half, width), lambda i: (0, i, 0, 0)),
        scratch_shapes=[pltpu.VMEM((events, 2 * width), jnp.bfloat16)],
        cost_estimate=pl.CostEstimate(
            flops=4 * heavy * events * width, bytes_accessed=4 * events * width, transcendentals=0
        ),
        compiler_params=pltpu.CompilerParams(dimension_semantics=("arbitrary",)),
        name="heavy",
    )(values, keys2d, heavy_wide)


def light_kernel(base_ref, got, out, rhs, rows):
    blocks = got.shape[0]
    width = got.shape[2]

    @pl.when(pl.program_id(0) == 0)
    def _():
        lane = lax.broadcasted_iota(jnp.int32, (1, LANES), 1)
        base = base_ref[0]

        @pl.loop(0, blocks // 2)
        def _(b):
            even = got[2 * b]
            odd = got[2 * b + 1]
            pair = jnp.concatenate([even[:CAP], odd[:CAP]], axis=0)
            rhs[pl.ds(pl.multiple_of(b * 2 * CAP, 2 * CAP), 2 * CAP), :] = split_bf16(pair)
            key = jnp.where(lane < CAP, even[CAP : CAP + 1], odd[CAP : CAP + 1])
            rows[pl.ds(b, 1), :] = key.astype(jnp.int32) - base

    tile = out.shape[0]
    mine = lax.broadcasted_iota(jnp.int32, (tile, LANES), 0) + pl.program_id(0) * tile
    acc = jnp.zeros((tile, 2 * width), jnp.float32)
    per = math.gcd(8, blocks // 2)
    step_k = per * LANES

    def body(s, acc):
        pieces = []
        for c in range(per):
            row = rows[pl.ds(s * per + c, 1), :]
            pieces.append(jnp.where(mine == row, 1.0, 0.0).astype(jnp.bfloat16))
        onehot = jnp.concatenate(pieces, axis=1)
        at = pl.ds(pl.multiple_of(s * step_k, step_k), step_k)
        return acc + jnp.dot(onehot, rhs[at, :], preferred_element_type=jnp.float32)

    acc = lax.fori_loop(0, blocks * CAP // step_k, body, acc)
    out[...] = acc[:, :width] + acc[:, width:]


def light_totals(got, base, keys_dev):
    blocks, unused, width = got.shape
    tile = 256
    return pl.pallas_call(
        light_kernel,
        out_shape=jax.ShapeDtypeStruct((keys_dev, width), jnp.float32),
        grid=(keys_dev // tile,),
        in_specs=[
            pl.BlockSpec(memory_space=pltpu.SMEM),
            pl.BlockSpec(got.shape, lambda i: (0, 0, 0), pipeline_mode=pl.Buffered(1)),
        ],
        out_specs=pl.BlockSpec((tile, width), lambda i: (i, 0)),
        scratch_shapes=[
            pltpu.VMEM((blocks * CAP, 2 * width), jnp.bfloat16),
            pltpu.VMEM((blocks // 2, LANES), jnp.int32),
        ],
        cost_estimate=pl.CostEstimate(
            flops=4 * keys_dev * blocks * CAP * width,
            bytes_accessed=4 * keys_dev * width,
            transcendentals=0,
        ),
        compiler_params=pltpu.CompilerParams(dimension_semantics=("arbitrary",)),
        name="light",
    )(base, got)


KEYS_DEV = 4096


def per_device(values, key_ids, heavy_ids, block_offsets, block_counts):
    owners = lax.axis_size("own")
    pairs = lax.axis_size("rep")
    own_index = lax.axis_index("own")
    events, width = values.shape
    keys2d = key_ids.reshape(events // LANES, LANES)
    payload = pack(values, keys2d, block_offsets, block_counts, owners)
    payload = jnp.concatenate([payload] * pairs, axis=0)
    got = lax.all_to_all(payload, ("rep", "own"), split_axis=0, concat_axis=0, tiled=True)
    heavy_wide = jnp.broadcast_to(heavy_ids[:, None], (heavy_ids.shape[0], LANES))
    partial = heavy_partials(values, keys2d, heavy_wide, pairs, owners)
    partial = partial.reshape((pairs * owners,) + partial.shape[2:])
    swapped = lax.all_to_all(partial, ("rep", "own"), split_axis=0, concat_axis=0, tiled=True)
    base = (own_index * KEYS_DEV).astype(jnp.int32).reshape(1)
    light_sums = light_totals(got, base, KEYS_DEV)
    mine = jnp.sum(swapped, axis=0)
    heavy_sums = lax.all_gather(mine, "rep", axis=0, tiled=True)
    return (light_sums, heavy_sums)


def solution(mesh):
    placed = (
        P(("rep", "own"), None),
        P(("rep", "own")),
        P(),
        P(("rep", "own"), None),
        P(("rep", "own"), None),
    )
    return jax.shard_map(
        per_device,
        mesh=mesh,
        in_specs=placed,
        out_specs=(P("own", None), P("own", None)),
        check_vma=False,
    )
```

time: 166 us -> 109 us (0.66)
  matrix products: 42.9 us -> 0 us
  Pallas kernels: 0 us -> 41.9 us
  waiting for transfers between devices: 69.8 us -> 41.5 us
  local copies, waits for them, and re-layouts: 20.6 us -> 3.65 us
  between operations: 15.6 us -> 0.67 us
  blocking collectives: 0 us -> 8.41 us
  starting transfers between devices: 13.5 us -> 9.98 us
    reduce_scatter x1 -> x0, waiting for transfers between devices: 49.9 us -> none  [per_device(): lax.psum_scatter(summed_pair, 'own', scatter_dimension=0, tiled=True)]
    dot_general x5 -> x0, matrix products: 42.9 us -> none  [accumulate(): jnp.dot(onehot, rows_piece, precision=lax.Precision.HIGHEST, preferred_el...]
    pallas_call x0 -> x3, Pallas kernels: none -> 41.9 us  [the longest x1 24 us: heavy_partials(): pl.pallas_call(functools.partial(heavy_kernel, 1024, pairs, rows_owner),...]
    all_to_all x2, waiting for transfers between devices: 0.01 us -> 41.5 us  [the longest x1 21.5 us: per_device(): lax.all_to_all(payload, ('rep', 'own'), split_axis=0, concat_axis=0, tile...]
    psum x1 -> x0, waiting for transfers between devices: 19.8 us -> none  [per_device(): summed_pair = lax.psum(partial_sums, 'rep')]
    gather x4 -> x0, local copies, waits for them, and re-layouts: 11.3 us -> none  [the longest x3 6.28 us: per_device(): block_keys = jnp.where(valid, jnp.take(padded_keys, positions, axis=0), -1)]
    all_gather x0 -> x1, blocking collectives: none -> 8.41 us  [per_device(): heavy_sums = lax.all_gather(mine, 'rep', axis=0, tiled=True)]
    concatenate x2 -> x0, local copies, waits for them, and re-layouts: 4.47 us -> none  [the longest x1 3.71 us: per_device(): jnp.concatenate([values, jnp.zeros((slot_cap, width), jnp.float32)], axis=0)]
  transfers between devices with their start and end apart: 5 -> 2, of which waited for: 2 -> 2; matrix products, arithmetic and copies ran while one was open for 32% -> 2% of each run, Pallas kernels for 0% -> 4%
where the time goes in v1:
time: 109 us; the launch traced here: 108 us
  Pallas kernels  41.9 us (38%)
  waiting for transfers between devices  41.5 us (38%)
  starting transfers between devices  9.98 us (9%)
  blocking collectives  8.41 us (8%)
  local copies, waits for them, and re-layouts  3.65 us (3%)
  other arithmetic  2.4 us (2%)
    pallas_call x1, Pallas kernels, heavy_partials(): pl.pallas_call(functools.partial(heavy_kernel, 1024, pairs, rows_owner),...  24 us
    all_to_all x1, waiting for transfers between devices, per_device(): lax.all_to_all(payload, ('rep', 'own'), split_axis=0, concat_axis=0, tile...  21.5 us
    all_to_all x1, waiting for transfers between devices, per_device(): lax.all_to_all(partial, ('rep', 'own'), split_axis=0, concat_axis=0, tile...  20 us
    pallas_call x1, Pallas kernels, light_totals(): pl.pallas_call(light_kernel, out_shape=jax.ShapeDtypeStruct((keys_dev, wi...  13 us
    all_gather x1, blocking collectives, per_device(): heavy_sums = lax.all_gather(mine, 'rep', axis=0, tiled=True)  8.41 us
    all_to_all x1, starting transfers between devices, per_device(): lax.all_to_all(partial, ('rep', 'own'), split_axis=0, concat_axis=0, tile...  7.33 us
    pallas_call x1, Pallas kernels, pack(): pl.pallas_call(functools.partial(pack_kernel, owners, events), out_shape=...  4.86 us
    all_to_all x1, starting transfers between devices, per_device(): lax.all_to_all(payload, ('rep', 'own'), split_axis=0, concat_axis=0, tile...  2.66 us
  transfers between devices with their start and end apart: 2, of which 2 were waited for; matrix products, arithmetic and copies ran while one was open for 2% of the time, Pallas kernels for 4%

profile of v1, /device:TPU:0, one launch (start us, length us, event | category | flops | bytes accessed | tf_op | source)
XLA Modules:
  0.0 108.4 jit_solution(4848260195832383970)
XLA Ops:
  0.6 2.0 %broadcast_in_dim.2.heavy = s32[2048,128]{1,0:T(8,128)} broadcast(s32[2048]{0:T(1024)} %param.7), dimensions={0} | broadcast | bytes 1056768 | tf_op jit(solution)/shard_map/broadcast_in_dim | solution.py:209
  2.6 24.0 %heavy.1 = f32[2,16,64,128]{3,2,1,0:T(8,128)} custom-call(f32[8192,128]{1,0:T(8,128)} %vals.3, s32[64,128]{1,0:T(8,128)} %bitcast.4, s32[2048,128]{1,0:T(8,128)} %broadcast_in_dim.2.heavy), custom_call_target="tpu_custom_call" | custom-call | flops 8589934592 | bytes 4194304 | tf_op jit(solution)/shard_map/heavy/pallas_call | solution.py:115
  26.6 7.3 %all-to-all-start.1 = ((f32[32,64,128]{2,1,0:T(8,128)}), f32[32,64,128]{2,1,0:T(8,128)S(1)}, u32[]{:S(2)}, u32[]{:S(2)}) async-start(f32[32,64,128]{2,1,0:T(8,128)} %bitcast.3), calls=%async_computation.1 | async-start | bytes 2097152 | tf_op jit(solution)/shard_map/all_to_all | solution.py:212
  33.9 4.9 %pack.1 = f32[16,72,128]{2,1,0:T(8,128)} custom-call(s32[1,16]{1,0:T(1,128)} %offs.1, s32[1,16]{1,0:T(1,128)} %cnts.1, f32[8192,128]{1,0:T(8,128)} %vals.3, s32[64,128]{1,0:T(8,128)} %bitcast.5), custom_call_target="tpu_custom_call" | custom-call | tf_op jit(solution)/shard_map/pack/pallas_call | solution.py:61
  38.8 2.3 %pad_maximum_fusion = f32[32,72,128]{2,1,0:T(8,128)} fusion(f32[16,72,128]{2,1,0:T(8,128)} %pack.1), kind=kLoop, calls=%fused_computation | loop fusion | flops 294912 | bytes 1769472 | tf_op jit(solution)/shard_map/concatenate | solution.py:207
  41.1 20.0 %all-to-all-done.1 = f32[32,64,128]{2,1,0:T(8,128)S(1)} async-done(((f32[32,64,128]{2,1,0:T(8,128)}), f32[32,64,128]{2,1,0:T(8,128)S(1)}, u32[]{:S(2)}, u32[]{:S(2)}) %all-to-all-start.1) | async-done | bytes 1048608 | tf_op jit(solution)/shard_map/all_to_all | solution.py:212
  61.1 2.7 %all-to-all-start = ((f32[32,72,128]{2,1,0:T(8,128)}), f32[32,72,128]{2,1,0:T(8,128)S(1)}, u32[]{:S(2)}, u32[]{:S(2)}) async-start(f32[32,72,128]{2,1,0:T(8,128)} %pad_maximum_fusion), calls=%async_computation | async-start | bytes 2359296 | tf_op jit(solution)/shard_map/all_to_all | solution.py:208
  63.8 0.1 reduce_sum.9
  63.8 8.4 %all_gather.3 = f32[128,128]{1,0:T(8,128)S(1)} all-gather(f32[64,128]{1,0:T(8,128)S(1)} %reduce_sum.9), channel_id=1, replica_groups=mesh['rep'=2,'own'=16] {'rep'}, dimensions={0}, use_global_device_ids=true | all-gather | bytes 98304 | tf_op jit(solution)/shard_map/all_gather | solution.py:216
  72.3 21.5 %all-to-all-done.got = f32[32,72,128]{2,1,0:T(8,128)S(1)} async-done(((f32[32,72,128]{2,1,0:T(8,128)}), f32[32,72,128]{2,1,0:T(8,128)S(1)}, u32[]{:S(2)}, u32[]{:S(2)}) %all-to-all-start) | async-done | bytes 1179680 | tf_op jit(solution)/shard_map/all_to_all | solution.py:208
  93.7 0.0 copy-start
  93.7 1.0 copy-done
  94.8 13.0 %light.1 = f32[4096,128]{1,0:T(8,128)} custom-call(s32[1]{0:T(128)} %bitcast.base_ref, f32[32,72,128]{2,1,0:T(8,128)} %copy-done), custom_call_target="tpu_custom_call" | custom-call | flops 4294967296 | bytes 2097152 | tf_op jit(solution)/shard_map/light/pallas_call | solution.py:174
  107.8 0.6 copy.8
Async XLA Ops:
  26.6 34.5 %all-to-all-start.1 = ((f32[32,64,128]{2,1,0:T(8,128)}), f32[32,64,128]{2,1,0:T(8,128)S(1)}, u32[]{:S(2)}, u32[]{:S(2)}) async-start(f32[32,64,128]{2,1,0:T(8,128)} %bitcast.3), calls=%async_computation.1 | async-start | bytes 2097152 | tf_op jit(solution)/shard_map/all_to_all | solution.py:212
  61.1 32.6 %all-to-all-start = ((f32[32,72,128]{2,1,0:T(8,128)}), f32[32,72,128]{2,1,0:T(8,128)S(1)}, u32[]{:S(2)}, u32[]{:S(2)}) async-start(f32[32,72,128]{2,1,0:T(8,128)} %pad_maximum_fusion), calls=%async_computation | async-start | bytes 2359296 | tf_op jit(solution)/shard_map/all_to_all | solution.py:208
  93.7 1.0 copy-start

commit v2 on v1

--- a/solution.py
+++ b/solution.py
@@ -10,6 +10,7 @@
 
 CAP = 64
 LANES = 128
+MESH = pl.DeviceIdType.MESH
 
 
 def split_bf16(rows):
@@ -71,64 +72,262 @@
     )(offsets, counts, values, keys2d)
 
 
-def heavy_kernel(step_k, pairs, rows_owner, vals, keys, heavy, out, rhs):
-    events = vals.shape[0]
+def exchange_kernel(
+    pairs, owners, step_k, payload, vals, keys, heavy, got, sums_out,
+    staged, rhs, part, quad, mine, landed, final,
+    vs, ls, lr, fs, fr, qs, qr, ts, tr, es, er,
+):
+    r = lax.axis_index("rep")
+    own = lax.axis_index("own")
+    core = lax.rem(own, 2)
+    chip = lax.div(own, 2)
+    chips = owners // 2
+    events, width = vals.shape
     steps = events // step_k
-    chunk = heavy.shape[0]
+    chunk = heavy.shape[0] // chips
+    rows_owner = chunk // 2
     half = rows_owner // pairs
-
-    @pl.when(pl.program_id(0) == 0)
-    def _():
-        @pl.loop(0, steps)
-        def _(s):
-            at = pl.ds(pl.multiple_of(s * step_k, step_k), step_k)
-            rhs[at, :] = split_bf16(vals[at, :])
-
-    targets = heavy[...]
-    acc = jnp.zeros((chunk, rhs.shape[1]), jnp.float32)
-
-    def body(s, acc):
+    members = 2 * pairs
+
+    def value_copy(s):
         at = pl.ds(pl.multiple_of(s * step_k, step_k), step_k)
-        pieces = []
-        for c in range(step_k // LANES):
-            row = keys[pl.ds(s * (step_k // LANES) + c, 1), :]
-            pieces.append(jnp.where(targets == row, 1.0, 0.0).astype(jnp.bfloat16))
-        onehot = jnp.concatenate(pieces, axis=1)
-        return acc + jnp.dot(onehot, rhs[at, :], preferred_element_type=jnp.float32)
-
-    acc = lax.fori_loop(0, steps, body, acc)
-    width = vals.shape[1]
-    sums = acc[:, :width] + acc[:, width:]
-    for o in range(chunk // rows_owner):
-        for r in range(pairs):
-            begin = o * rows_owner + r * half
-            out[r, o] = sums[begin : begin + half]
-
-
-def heavy_partials(values, keys2d, heavy_wide, pairs, owners):
+        return pltpu.make_async_copy(vals.at[at], staged.at[at], vs.at[s])
+
+    for s in range(steps):
+        value_copy(s).start()
+
+    barrier = pltpu.get_barrier_semaphore()
+
+    @pl.loop(1, owners)
+    def _(d):
+        pl.semaphore_signal(
+            barrier, 1, device_id=(r, lax.rem(own + d, owners)), device_id_type=MESH
+        )
+
+    for m in range(2, members):
+        pl.semaphore_signal(
+            barrier, 1,
+            device_id=(lax.rem(r + m // 2, pairs), 2 * chip + lax.rem(core + m, 2)),
+            device_id_type=MESH,
+        )
+    pl.semaphore_wait(barrier, owners - 1 + members - 2)
+
+    def light(d):
+        dest = lax.rem(own + d, owners)
+        return pltpu.make_async_remote_copy(
+            src_ref=payload.at[dest], dst_ref=got.at[r * owners + own],
+            send_sem=ls.at[d], recv_sem=lr.at[d],
+            device_id=(r, dest), device_id_type=MESH,
+        )
+
+    here = pltpu.make_async_copy(payload.at[own], got.at[r * owners + own], ls.at[0])
+    here.start()
+
+    @pl.loop(1, owners)
+    def _(d):
+        light(d).start()
+
+    def forward(d, q):
+        slot = r * owners + lax.rem(own - d + owners, owners)
+        return pltpu.make_async_remote_copy(
+            src_ref=got.at[slot], dst_ref=got.at[slot],
+            send_sem=fs.at[q - 1, d], recv_sem=fr.at[q - 1, d],
+            device_id=(lax.rem(r + q, pairs), own), device_id_type=MESH,
+        )
+
+    def gather_quad(c, m):
+        peer_r = lax.rem(r + m // 2, pairs)
+        peer_k = lax.rem(core + m, 2)
+        return pltpu.make_async_remote_copy(
+            src_ref=part.at[c, peer_r, peer_k], dst_ref=quad.at[c, m - 1],
+            send_sem=qs.at[c, m - 1], recv_sem=qr.at[c, m - 1],
+            device_id=(peer_r, 2 * chip + peer_k), device_id_type=MESH,
+        )
+
+    def deliver(c):
+        return pltpu.make_async_remote_copy(
+            src_ref=mine.at[c], dst_ref=landed.at[chip],
+            send_sem=ts.at[c], recv_sem=tr.at[chip],
+            device_id=(r, 2 * c + core), device_id_type=MESH,
+        )
+
+    def arrival(c):
+        return pltpu.make_async_remote_copy(
+            src_ref=mine.at[c], dst_ref=landed.at[c],
+            send_sem=ts.at[c], recv_sem=tr.at[c],
+            device_id=(r, 2 * c + core), device_id_type=MESH,
+        )
+
+    for s in range(steps):
+        value_copy(s).wait()
+        rhs[s * step_k : (s + 1) * step_k, :] = split_bf16(staged[s * step_k : (s + 1) * step_k, :])
+
+    group = owners // (chips // 2)
+    first_forward = chips - chips // 2
+
+    def chunk_at(i):
+        return lax.rem(chip + 1 + i, chips)
+
+    @pl.loop(0, chips + 4)
+    def _(i):
+        @pl.when(i < chips)
+        def _():
+            c = chunk_at(i)
+            targets = heavy[pl.ds(pl.multiple_of(c * chunk, chunk), chunk), :]
+
+            def body(s, acc):
+                at = pl.ds(pl.multiple_of(s * step_k, step_k), step_k)
+                pieces = []
+                for p in range(step_k // LANES):
+                    row = keys[pl.ds(s * (step_k // LANES) + p, 1), :]
+                    pieces.append(jnp.where(targets == row, 1.0, 0.0).astype(jnp.bfloat16))
+                onehot = jnp.concatenate(pieces, axis=1)
+                return acc + jnp.dot(onehot, rhs[at, :], preferred_element_type=jnp.float32)
+
+            acc = lax.fori_loop(0, steps, body, jnp.zeros((chunk, 2 * width), jnp.float32))
+            sums = acc[:, :width] + acc[:, width:]
+            for k in range(2):
+                for side in range(pairs):
+                    begin = k * rows_owner + side * half
+                    part[c, side, k] = sums[begin : begin + half]
+
+        @pl.when((i >= 1) & (i < chips + 1))
+        def _():
+            c = chunk_at(i - 1)
+            for m in range(1, members):
+                gather_quad(c, m).start()
+
+        @pl.when((i >= first_forward) & (i < chips))
+        def _():
+            for g in range(group):
+                d = (i - first_forward) * group + g
+
+                @pl.when(d == 0)
+                def _():
+                    here.wait()
+
+                @pl.when(d > 0)
+                def _():
+                    light(d).wait_recv()
+
+                for q in range(1, pairs):
+                    forward(d, q).start()
+
+        @pl.when((i >= 4) & (i < chips + 4))
+        def _():
+            c = chunk_at(i - 4)
+
+            @pl.when(c != chip)
+            def _():
+                deliver(c).start()
+
+        @pl.when((i >= 3) & (i < chips + 3))
+        def _():
+            c = chunk_at(i - 3)
+            total = part[c, r, core]
+            for m in range(1, members):
+                gather_quad(c, m).wait_recv()
+                total = total + quad[c, m - 1]
+            mine[c] = total
+
+    total = mine[chip]
+    for j in range(1, chips):
+        c = lax.rem(chip + chips - j, chips)
+        arrival(c).wait_recv()
+        total = total + landed[c]
+    final[r] = total
+
+    @pl.loop(0, owners)
+    def _(d):
+        for q in range(1, pairs):
+            forward(d, q).wait_recv()
+
+        @pl.when(d > 0)
+        def _():
+            light(d).wait_send()
+
+    def share(q):
+        return pltpu.make_async_remote_copy(
+            src_ref=final.at[r], dst_ref=final.at[r],
+            send_sem=es.at[q - 1], recv_sem=er.at[q - 1],
+            device_id=(lax.rem(r + q, pairs), own), device_id_type=MESH,
+        )
+
+    for q in range(1, pairs):
+        share(q).start()
+
+    @pl.loop(0, owners)
+    def _(d):
+        for q in range(1, pairs):
+            forward(d, q).wait_send()
+
+    @pl.loop(0, chips)
+    def _(c):
+        for m in range(1, members):
+            gather_quad(c, m).wait_send()
+
+        @pl.when(c != chip)
+        def _():
+            deliver(c).wait_send()
+
+    for q in range(1, pairs):
+        back = lax.rem(r - q + pairs, pairs)
+        pltpu.make_async_remote_copy(
+            src_ref=final.at[back], dst_ref=final.at[back],
+            send_sem=es.at[q - 1], recv_sem=er.at[q - 1],
+            device_id=(lax.rem(r + q, pairs), own), device_id_type=MESH,
+        ).wait_recv()
+        share(q).wait_send()
+    for side in range(pairs):
+        sums_out[side * half : (side + 1) * half, :] = final[side]
+
+
+def exchange(payload, values, keys2d, heavy_wide, pairs, owners):
     events, width = values.shape
     heavy = heavy_wide.shape[0]
     rows_owner = heavy // owners
-    chunk = max(rows_owner, min(256, heavy))
-    per = chunk // rows_owner
     half = rows_owner // pairs
+    chips = owners // 2
+    step_k = 1024
+    vmem = pl.BlockSpec(memory_space=pltpu.VMEM)
+    dma = pltpu.SemaphoreType.DMA
+    members = 2 * pairs
     return pl.pallas_call(
-        functools.partial(heavy_kernel, 1024, pairs, rows_owner),
-        out_shape=jax.ShapeDtypeStruct((pairs, owners, half, width), jnp.float32),
-        grid=(heavy // chunk,),
-        in_specs=[
-            pl.BlockSpec((events, width), lambda i: (0, 0), pipeline_mode=pl.Buffered(1)),
-            pl.BlockSpec(keys2d.shape, lambda i: (0, 0), pipeline_mode=pl.Buffered(1)),
-            pl.BlockSpec((chunk, LANES), lambda i: (i, 0)),
+        functools.partial(exchange_kernel, pairs, owners, step_k),
+        out_shape=(
+            jax.ShapeDtypeStruct((pairs * owners, CAP + 8, width), jnp.float32),
+            jax.ShapeDtypeStruct((rows_owner, width), jnp.float32),
+        ),
+        in_specs=[vmem, pl.BlockSpec(memory_space=pl.ANY), vmem, vmem],
+        out_specs=(vmem, vmem),
+        scratch_shapes=[
+            pltpu.VMEM((events, width), jnp.float32),
+            pltpu.VMEM((events, 2 * width), jnp.bfloat16),
+            pltpu.VMEM((chips, pairs, 2, half, width), jnp.float32),
+            pltpu.VMEM((chips, members - 1, half, width), jnp.float32),
+            pltpu.VMEM((chips, half, width), jnp.float32),
+            pltpu.VMEM((chips, half, width), jnp.float32),
+            pltpu.VMEM((pairs, half, width), jnp.float32),
+            dma((events // step_k,)),
+            dma((owners,)),
+            dma((owners,)),
+            dma((pairs - 1, owners)),
+            dma((pairs - 1, owners)),
+            dma((chips, members - 1)),
+            dma((chips, members - 1)),
+            dma((chips,)),
+            dma((chips,)),
+            dma((pairs - 1,)),
+            dma((pairs - 1,)),
         ],
-        out_specs=pl.BlockSpec((pairs, per, half, width), lambda i: (0, i, 0, 0)),
-        scratch_shapes=[pltpu.VMEM((events, 2 * width), jnp.bfloat16)],
         cost_estimate=pl.CostEstimate(
             flops=4 * heavy * events * width, bytes_accessed=4 * events * width, transcendentals=0
         ),
-        compiler_params=pltpu.CompilerParams(dimension_semantics=("arbitrary",)),
-        name="heavy",
-    )(values, keys2d, heavy_wide)
+        compiler_params=pltpu.CompilerParams(
+            collective_id=0, has_side_effects=True, vmem_limit_bytes=50 * 1024 * 1024
+        ),
+        name="exchange",
+    )(payload, values, keys2d, heavy_wide)
 
 
 def light_kernel(base_ref, got, out, rhs, rows):
@@ -204,16 +403,10 @@
     events, width = values.shape
     keys2d = key_ids.reshape(events // LANES, LANES)
     payload = pack(values, keys2d, block_offsets, block_counts, owners)
-    payload = jnp.concatenate([payload] * pairs, axis=0)
-    got = lax.all_to_all(payload, ("rep", "own"), split_axis=0, concat_axis=0, tiled=True)
     heavy_wide = jnp.broadcast_to(heavy_ids[:, None], (heavy_ids.shape[0], LANES))
-    partial = heavy_partials(values, keys2d, heavy_wide, pairs, owners)
-    partial = partial.reshape((pairs * owners,) + partial.shape[2:])
-    swapped = lax.all_to_all(partial, ("rep", "own"), split_axis=0, concat_axis=0, tiled=True)
+    got, heavy_sums = exchange(payload, values, keys2d, heavy_wide, pairs, owners)
     base = (own_index * KEYS_DEV).astype(jnp.int32).reshape(1)
     light_sums = light_totals(got, base, KEYS_DEV)
-    mine = jnp.sum(swapped, axis=0)
-    heavy_sums = lax.all_gather(mine, "rep", axis=0, tiled=True)
     return (light_sums, heavy_sums)
 
 

time: 109 us -> 67.5 us (0.62)
  waiting for transfers between devices: 41.5 us -> 0 us
  Pallas kernels: 41.9 us -> 63.4 us
  starting transfers between devices: 9.98 us -> 0 us
  blocking collectives: 8.41 us -> 0 us
  other arithmetic: 2.4 us -> 0 us
    all_to_all x2 -> x0, waiting for transfers between devices: 41.5 us -> none  [the longest x1 21.5 us: per_device(): lax.all_to_all(payload, ('rep', 'own'), split_axis=0, concat_axis=0, tile...]
    pallas_call x1, Pallas kernels: 24 us -> 45.5 us  [exchange(): pl.pallas_call(functools.partial(exchange_kernel, pairs, owners, step_k),...]
    all_to_all x2 -> x0, starting transfers between devices: 9.98 us -> none  [the longest x1 7.33 us: per_device(): lax.all_to_all(partial, ('rep', 'own'), split_axis=0, concat_axis=0, tile...]
    all_gather x1 -> x0, blocking collectives: 8.41 us -> none  [per_device(): heavy_sums = lax.all_gather(mine, 'rep', axis=0, tiled=True)]
    concatenate x1 -> x0, other arithmetic: 2.33 us -> none  [per_device(): payload = jnp.concatenate([payload] * pairs, axis=0)]
    broadcast_in_dim x1, local copies, waits for them, and re-layouts: 2 us -> 0.32 us  [per_device(): jnp.broadcast_to(heavy_ids[:, None], (heavy_ids.shape[0], LANES))]
    unnamed x3 -> x9, local copies, waits for them, and re-layouts: 1.65 us -> 2.71 us
  transfers between devices with their start and end apart: 2 -> 0, of which waited for: 2 -> 0; matrix products, arithmetic and copies ran while one was open for 2% -> 0% of each run, Pallas kernels for 4% -> 0%
where the time goes in v2:
time: 67.5 us; the launch traced here: 67.2 us
  Pallas kernels  63.4 us (94%)
  local copies, waits for them, and re-layouts  3.03 us (4%)
  between operations  0.71 us (1%)
    pallas_call x1, Pallas kernels, exchange(): pl.pallas_call(functools.partial(exchange_kernel, pairs, owners, step_k),...  45.5 us
    pallas_call x1, Pallas kernels, light_totals(): pl.pallas_call(light_kernel, out_shape=jax.ShapeDtypeStruct((keys_dev, wi...  13 us
    pallas_call x1, Pallas kernels, pack(): pl.pallas_call(functools.partial(pack_kernel, owners, events), out_shape=...  4.91 us
    unnamed x9, local copies, waits for them, and re-layouts  2.71 us

profile of v2, /device:TPU:0, one launch (start us, length us, event | category | flops | bytes accessed | tf_op | source)
XLA Modules:
  0.0 67.2 jit_solution(13221312369460813713)
XLA Ops:
  0.6 0.0 copy-start.3
  0.6 0.0 copy-start.1
  0.7 4.9 %pack.1.payload = f32[16,72,128]{2,1,0:T(8,128)} custom-call(s32[1,16]{1,0:T(1,128)} %offs.1, s32[1,16]{1,0:T(1,128)} %cnts.1, f32[8192,128]{1,0:T(8,128)} %vals.3, s32[64,128]{1,0:T(8,128)} %bitcast.2), custom_call_target="tpu_custom_call" | custom-call | tf_op jit(solution)/shard_map/pack/pallas_call | solution.py:62
  5.6 0.0 copy-done.3
  5.6 0.3 broadcast_in_dim.2.heavy
  5.9 0.0 copy-done.1
  5.9 0.0 copy-start
  5.9 1.1 %copy-done = f32[16,72,128]{2,1,0:T(8,128)S(1)} copy-done((f32[16,72,128]{2,1,0:T(8,128)S(1)}, f32[16,72,128]{2,1,0:T(8,128)}, u32[]{:S(2)}) %copy-start) | copy-done | bytes 589848
  7.0 45.5 %exchange.1 = (f32[32,72,128]{2,1,0:T(8,128)S(1)}, f32[128,128]{1,0:T(8,128)S(1)}) custom-call(f32[16,72,128]{2,1,0:T(8,128)S(1)} %copy-done, f32[8192,128]{1,0:T(8,128)} %vals.3, s32[64,128]{1,0:T(8,128)S(1)} %bitcast.3, s32[2048,128]{1,0:T(8,128)S(1)} %broadcast_in_dim.2.heavy), custom_call_target="tpu_custom_call" | custom-call | flops 8589934592 | bytes 4194304 | tf_op jit(solution)/shard_map/exchange/pallas_call | solution.py:295
  52.5 0.0 copy-start.2
  52.5 1.0 %copy-done.2 = f32[32,72,128]{2,1,0:T(8,128)} copy-done((f32[32,72,128]{2,1,0:T(8,128)}, f32[32,72,128]{2,1,0:T(8,128)S(1)}, u32[]{:S(2)}) %copy-start.2) | copy-done | bytes 1179672
  53.5 13.0 %light.1 = f32[4096,128]{1,0:T(8,128)} custom-call(s32[1]{0:T(128)} %bitcast.base_ref, f32[32,72,128]{2,1,0:T(8,128)} %copy-done.2), custom_call_target="tpu_custom_call" | custom-call | flops 4294967296 | bytes 2097152 | tf_op jit(solution)/shard_map/light/pallas_call | solution.py:373
  66.5 0.6 copy.8
Async XLA Ops:
  0.6 4.9 %copy-start.3 = (s32[2048]{0:T(1024)S(1)}, s32[2048]{0:T(1024)}, u32[]{:S(2)}) copy-start(s32[2048]{0:T(1024)} %param.7) | copy-start | bytes 24580
  0.6 5.3 %copy-start.1 = (s32[8192]{0:T(1024)S(1)}, s32[8192]{0:T(1024)}, u32[]{:S(2)}) copy-start(s32[8192]{0:T(1024)} %param.6) | copy-start | bytes 98308
  5.9 1.1 %copy-start = (f32[16,72,128]{2,1,0:T(8,128)S(1)}, f32[16,72,128]{2,1,0:T(8,128)}, u32[]{:S(2)}) copy-start(f32[16,72,128]{2,1,0:T(8,128)} %pack.1.payload) | copy-start | bytes 1769476
  52.5 1.0 %copy-start.2 = (f32[32,72,128]{2,1,0:T(8,128)}, f32[32,72,128]{2,1,0:T(8,128)S(1)}, u32[]{:S(2)}) copy-start(f32[32,72,128]{2,1,0:T(8,128)S(1)} %get-tuple-element.4.got) | copy-start | bytes 3538948

commit v3 on v2

--- a/solution.py
+++ b/solution.py
@@ -23,23 +23,27 @@
     def start_of(o):
         return jnp.minimum(offs[0, o], events - CAP)
 
+    def base_of(o):
+        return pl.multiple_of(jnp.minimum((start_of(o) // 8) * 8, events - CAP - 8), 8)
+
     def copy_of(o):
-        base = pl.multiple_of(jnp.minimum((start_of(o) // 8) * 8, events - CAP - 8), 8)
-        return base, pltpu.make_async_copy(
-            vals.at[pl.ds(base, CAP + 8)], stage.at[o], sems.at[o]
+        return pltpu.make_async_copy(
+            vals.at[pl.ds(base_of(o), CAP + 8)], stage.at[o], sems.at[o]
         )
 
     @pl.loop(0, owners)
     def _(o):
-        copy_of(o)[1].start()
+        copy_of(o).start()
 
     lane = lax.broadcasted_iota(jnp.int32, (1, LANES), 1)
     last_row = events // LANES - 1
 
     @pl.loop(0, owners)
     def _(o):
-        base, copy = copy_of(o)
-        copy.wait()
+        copy_of(o).wait()
+
+    def fill(o):
+        base = base_of(o)
         start = start_of(o)
         skip = offs[0, o] - start
         out[o, 0:CAP, :] = stage[o, pl.ds(start - base, CAP), :]
@@ -53,6 +57,13 @@
         block = jnp.where(valid, joined, -1)
         twice = jnp.where(lane < CAP, block, pltpu.roll(block, CAP, 1))
         out[o, CAP : CAP + 8, :] = jnp.broadcast_to(twice, (8, LANES)).astype(jnp.float32)
+
+    unroll = math.gcd(owners, 8)
+
+    @pl.loop(0, owners // unroll)
+    def _(g):
+        for u in range(unroll):
+            fill(g * unroll + u)
 
 
 def pack(values, keys2d, offsets, counts, owners):
@@ -162,8 +173,8 @@
         value_copy(s).wait()
         rhs[s * step_k : (s + 1) * step_k, :] = split_bf16(staged[s * step_k : (s + 1) * step_k, :])
 
-    group = owners // (chips // 2)
-    first_forward = chips - chips // 2
+    group = owners // chips
+    first_forward = min(3, chips)
 
     def chunk_at(i):
         return lax.rem(chip + 1 + i, chips)
@@ -175,16 +186,12 @@
             c = chunk_at(i)
             targets = heavy[pl.ds(pl.multiple_of(c * chunk, chunk), chunk), :]
 
-            def body(s, acc):
-                at = pl.ds(pl.multiple_of(s * step_k, step_k), step_k)
-                pieces = []
-                for p in range(step_k // LANES):
-                    row = keys[pl.ds(s * (step_k // LANES) + p, 1), :]
-                    pieces.append(jnp.where(targets == row, 1.0, 0.0).astype(jnp.bfloat16))
-                onehot = jnp.concatenate(pieces, axis=1)
-                return acc + jnp.dot(onehot, rhs[at, :], preferred_element_type=jnp.float32)
-
-            acc = lax.fori_loop(0, steps, body, jnp.zeros((chunk, 2 * width), jnp.float32))
+            pieces = []
+            for p in range(events // LANES):
+                row = keys[p : p + 1, :]
+                pieces.append(jnp.where(targets == row, 1.0, 0.0).astype(jnp.bfloat16))
+            onehot = jnp.concatenate(pieces, axis=1)
+            acc = jnp.dot(onehot, rhs[...], preferred_element_type=jnp.float32)
             sums = acc[:, :width] + acc[:, width:]
             for k in range(2):
                 for side in range(pairs):
@@ -196,22 +203,6 @@
             c = chunk_at(i - 1)
             for m in range(1, members):
                 gather_quad(c, m).start()
-
-        @pl.when((i >= first_forward) & (i < chips))
-        def _():
-            for g in range(group):
-                d = (i - first_forward) * group + g
-
-                @pl.when(d == 0)
-                def _():
-                    here.wait()
-
-                @pl.when(d > 0)
-                def _():
-                    light(d).wait_recv()
-
-                for q in range(1, pairs):
-                    forward(d, q).start()
 
         @pl.when((i >= 4) & (i < chips + 4))
         def _():
@@ -229,6 +220,22 @@
                 gather_quad(c, m).wait_recv()
                 total = total + quad[c, m - 1]
             mine[c] = total
+
+        @pl.when((i >= first_forward) & (i < first_forward + chips))
+        def _():
+            for g in range(group):
+                d = (i - first_forward) * group + g
+
+                @pl.when(d == 0)
+                def _():
+                    here.wait()
+
+                @pl.when(d > 0)
+                def _():
+                    light(d).wait_recv()
+
+                for q in range(1, pairs):
+                    forward(d, q).start()
 
     total = mine[chip]
     for j in range(1, chips):
@@ -339,8 +346,7 @@
         lane = lax.broadcasted_iota(jnp.int32, (1, LANES), 1)
         base = base_ref[0]
 
-        @pl.loop(0, blocks // 2)
-        def _(b):
+        def stage(b):
             even = got[2 * b]
             odd = got[2 * b + 1]
             pair = jnp.concatenate([even[:CAP], odd[:CAP]], axis=0)
@@ -348,28 +354,27 @@
             key = jnp.where(lane < CAP, even[CAP : CAP + 1], odd[CAP : CAP + 1])
             rows[pl.ds(b, 1), :] = key.astype(jnp.int32) - base
 
+        unroll = math.gcd(blocks // 2, 4)
+
+        @pl.loop(0, blocks // 2 // unroll)
+        def _(g):
+            for u in range(unroll):
+                stage(g * unroll + u)
+
     tile = out.shape[0]
     mine = lax.broadcasted_iota(jnp.int32, (tile, LANES), 0) + pl.program_id(0) * tile
-    acc = jnp.zeros((tile, 2 * width), jnp.float32)
-    per = math.gcd(8, blocks // 2)
-    step_k = per * LANES
-
-    def body(s, acc):
-        pieces = []
-        for c in range(per):
-            row = rows[pl.ds(s * per + c, 1), :]
-            pieces.append(jnp.where(mine == row, 1.0, 0.0).astype(jnp.bfloat16))
-        onehot = jnp.concatenate(pieces, axis=1)
-        at = pl.ds(pl.multiple_of(s * step_k, step_k), step_k)
-        return acc + jnp.dot(onehot, rhs[at, :], preferred_element_type=jnp.float32)
-
-    acc = lax.fori_loop(0, blocks * CAP // step_k, body, acc)
+    pieces = []
+    for c in range(blocks // 2):
+        row = rows[c : c + 1, :]
+        pieces.append(jnp.where(mine == row, 1.0, 0.0).astype(jnp.bfloat16))
+    onehot = jnp.concatenate(pieces, axis=1)
+    acc = jnp.dot(onehot, rhs[...], preferred_element_type=jnp.float32)
     out[...] = acc[:, :width] + acc[:, width:]
 
 
 def light_totals(got, base, keys_dev):
     blocks, unused, width = got.shape
-    tile = 256
+    tile = math.gcd(keys_dev, 512)
     return pl.pallas_call(
         light_kernel,
         out_shape=jax.ShapeDtypeStruct((keys_dev, width), jnp.float32),

time: 67.5 us -> 54.7 us (0.81)
  Pallas kernels: 63.4 us -> 50.6 us
    pallas_call x1, Pallas kernels: 45.5 us -> 39.3 us  [exchange(): pl.pallas_call(functools.partial(exchange_kernel, pairs, owners, step_k),...]
    pallas_call x1, Pallas kernels: 13 us -> 7.95 us  [light_totals(): pl.pallas_call(light_kernel, out_shape=jax.ShapeDtypeStruct((keys_dev, wi...]
    pallas_call x1, Pallas kernels: 4.91 us -> 3.34 us  [pack(): pl.pallas_call(functools.partial(pack_kernel, owners, events), out_shape=...]
where the time goes in v3:
time: 54.7 us; the launch traced here: 54.4 us
  Pallas kernels  50.6 us (93%)
  local copies, waits for them, and re-layouts  3.03 us (6%)
  between operations  0.71 us (1%)
    pallas_call x1, Pallas kernels, exchange(): pl.pallas_call(functools.partial(exchange_kernel, pairs, owners, step_k),...  39.3 us
    pallas_call x1, Pallas kernels, light_totals(): pl.pallas_call(light_kernel, out_shape=jax.ShapeDtypeStruct((keys_dev, wi...  7.95 us
    pallas_call x1, Pallas kernels, pack(): pl.pallas_call(functools.partial(pack_kernel, owners, events), out_shape=...  3.34 us
    unnamed x9, local copies, waits for them, and re-layouts  2.71 us

profile of v3, /device:TPU:0, one launch (start us, length us, event | category | flops | bytes accessed | tf_op | source)
XLA Modules:
  0.0 54.4 jit_solution(10330413625572635010)
XLA Ops:
  0.6 0.0 copy-start.3
  0.6 0.0 copy-start.1
  0.7 3.3 %pack.1.payload = f32[16,72,128]{2,1,0:T(8,128)} custom-call(s32[1,16]{1,0:T(1,128)} %offs.1, s32[1,16]{1,0:T(1,128)} %cnts.1, f32[8192,128]{1,0:T(8,128)} %vals.3, s32[64,128]{1,0:T(8,128)} %bitcast.2), custom_call_target="tpu_custom_call" | custom-call | tf_op jit(solution)/shard_map/pack/pallas_call | solution.py:73
  4.0 0.0 copy-done.3
  4.0 0.3 broadcast_in_dim.2.heavy
  4.3 0.0 copy-done.1
  4.4 0.0 copy-start
  4.4 1.1 %copy-done = f32[16,72,128]{2,1,0:T(8,128)S(1)} copy-done((f32[16,72,128]{2,1,0:T(8,128)S(1)}, f32[16,72,128]{2,1,0:T(8,128)}, u32[]{:S(2)}) %copy-start) | copy-done | bytes 589848
  5.4 39.3 %exchange.1 = (f32[32,72,128]{2,1,0:T(8,128)S(1)}, f32[128,128]{1,0:T(8,128)S(1)}) custom-call(f32[16,72,128]{2,1,0:T(8,128)S(1)} %copy-done, f32[8192,128]{1,0:T(8,128)} %vals.3, s32[64,128]{1,0:T(8,128)S(1)} %bitcast.3, s32[2048,128]{1,0:T(8,128)S(1)} %broadcast_in_dim.2.heavy), custom_call_target="tpu_custom_call" | custom-call | flops 8589934592 | bytes 4194304 | tf_op jit(solution)/shard_map/exchange/pallas_call | solution.py:302
  44.8 0.0 copy-start.2
  44.8 1.0 %copy-done.2 = f32[32,72,128]{2,1,0:T(8,128)} copy-done((f32[32,72,128]{2,1,0:T(8,128)}, f32[32,72,128]{2,1,0:T(8,128)S(1)}, u32[]{:S(2)}) %copy-start.2) | copy-done | bytes 1179672
  45.8 8.0 %light.1 = f32[4096,128]{1,0:T(8,128)} custom-call(s32[1]{0:T(128)} %bitcast.base_ref, f32[32,72,128]{2,1,0:T(8,128)} %copy-done.2), custom_call_target="tpu_custom_call" | custom-call | flops 4294967296 | bytes 2097152 | tf_op jit(solution)/shard_map/light/pallas_call | solution.py:378
  53.8 0.6 %copy.8 = f32[128,128]{1,0:T(8,128)} copy(f32[128,128]{1,0:T(8,128)S(1)} %get-tuple-element.9) | data formatting | bytes 131072
Async XLA Ops:
  0.6 3.4 %copy-start.3 = (s32[2048]{0:T(1024)S(1)}, s32[2048]{0:T(1024)}, u32[]{:S(2)}) copy-start(s32[2048]{0:T(1024)} %param.7) | copy-start | bytes 24580
  0.6 3.7 %copy-start.1 = (s32[8192]{0:T(1024)S(1)}, s32[8192]{0:T(1024)}, u32[]{:S(2)}) copy-start(s32[8192]{0:T(1024)} %param.6) | copy-start | bytes 98308
  4.4 1.1 %copy-start = (f32[16,72,128]{2,1,0:T(8,128)S(1)}, f32[16,72,128]{2,1,0:T(8,128)}, u32[]{:S(2)}) copy-start(f32[16,72,128]{2,1,0:T(8,128)} %pack.1.payload) | copy-start | bytes 1769476
  44.8 1.0 %copy-start.2 = (f32[32,72,128]{2,1,0:T(8,128)}, f32[32,72,128]{2,1,0:T(8,128)S(1)}, u32[]{:S(2)}) copy-start(f32[32,72,128]{2,1,0:T(8,128)S(1)} %get-tuple-element.4.got) | copy-start | bytes 3538948

commit v4 on v3

--- a/solution.py
+++ b/solution.py
@@ -244,24 +244,24 @@
         total = total + landed[c]
     final[r] = total
 
+    @pl.loop(1, owners)
+    def _(d):
+        light(d).wait_send()
+
+    def share(q):
+        return pltpu.make_async_remote_copy(
+            src_ref=final.at[r], dst_ref=final.at[r],
+            send_sem=es.at[q - 1], recv_sem=er.at[q - 1],
+            device_id=(lax.rem(r + q, pairs), own), device_id_type=MESH,
+        )
+
+    for q in range(1, pairs):
+        share(q).start()
+
     @pl.loop(0, owners)
     def _(d):
         for q in range(1, pairs):
             forward(d, q).wait_recv()
-
-        @pl.when(d > 0)
-        def _():
-            light(d).wait_send()
-
-    def share(q):
-        return pltpu.make_async_remote_copy(
-            src_ref=final.at[r], dst_ref=final.at[r],
-            send_sem=es.at[q - 1], recv_sem=er.at[q - 1],
-            device_id=(lax.rem(r + q, pairs), own), device_id_type=MESH,
-        )
-
-    for q in range(1, pairs):
-        share(q).start()
 
     @pl.loop(0, owners)
     def _(d):

time: 54.7 us -> 53.1 us (0.971)
  Pallas kernels: 50.6 us -> 49 us
    pallas_call x1, Pallas kernels: 39.3 us -> 37.7 us  [exchange(): pl.pallas_call(functools.partial(exchange_kernel, pairs, owners, step_k),...]
where the time goes in v4:
time: 53.1 us; the launch traced here: 52.7 us
  Pallas kernels  49 us (92%)
  local copies, waits for them, and re-layouts  3.03 us (6%)
  between operations  0.71 us (1%)
    pallas_call x1, Pallas kernels, exchange(): pl.pallas_call(functools.partial(exchange_kernel, pairs, owners, step_k),...  37.7 us
    pallas_call x1, Pallas kernels, light_totals(): pl.pallas_call(light_kernel, out_shape=jax.ShapeDtypeStruct((keys_dev, wi...  7.95 us
    pallas_call x1, Pallas kernels, pack(): pl.pallas_call(functools.partial(pack_kernel, owners, events), out_shape=...  3.35 us
    unnamed x9, local copies, waits for them, and re-layouts  2.71 us

profile of v4, /device:TPU:0, one launch (start us, length us, event | category | flops | bytes accessed | tf_op | source)
XLA Modules:
  0.0 52.7 jit_solution(3902700803426651488)
XLA Ops:
  0.6 0.0 copy-start.3
  0.6 0.0 copy-start.1
  0.7 3.3 %pack.1.payload = f32[16,72,128]{2,1,0:T(8,128)} custom-call(s32[1,16]{1,0:T(1,128)} %offs.1, s32[1,16]{1,0:T(1,128)} %cnts.1, f32[8192,128]{1,0:T(8,128)} %vals.3, s32[64,128]{1,0:T(8,128)} %bitcast.2), custom_call_target="tpu_custom_call" | custom-call | tf_op jit(solution)/shard_map/pack/pallas_call | solution.py:73
  4.0 0.0 copy-done.3
  4.0 0.3 broadcast_in_dim.2.heavy
  4.4 0.0 copy-done.1
  4.4 0.0 copy-start
  4.4 1.1 %copy-done = f32[16,72,128]{2,1,0:T(8,128)S(1)} copy-done((f32[16,72,128]{2,1,0:T(8,128)S(1)}, f32[16,72,128]{2,1,0:T(8,128)}, u32[]{:S(2)}) %copy-start) | copy-done | bytes 589848
  5.4 37.7 %exchange.1 = (f32[32,72,128]{2,1,0:T(8,128)S(1)}, f32[128,128]{1,0:T(8,128)S(1)}) custom-call(f32[16,72,128]{2,1,0:T(8,128)S(1)} %copy-done, f32[8192,128]{1,0:T(8,128)} %vals.3, s32[64,128]{1,0:T(8,128)S(1)} %bitcast.3, s32[2048,128]{1,0:T(8,128)S(1)} %broadcast_in_dim.2.heavy), custom_call_target="tpu_custom_call" | custom-call | flops 8589934592 | bytes 4194304 | tf_op jit(solution)/shard_map/exchange/pallas_call | solution.py:302
  43.1 0.0 copy-start.2
  43.1 1.0 %copy-done.2 = f32[32,72,128]{2,1,0:T(8,128)} copy-done((f32[32,72,128]{2,1,0:T(8,128)}, f32[32,72,128]{2,1,0:T(8,128)S(1)}, u32[]{:S(2)}) %copy-start.2) | copy-done | bytes 1179672
  44.1 8.0 %light.1 = f32[4096,128]{1,0:T(8,128)} custom-call(s32[1]{0:T(128)} %bitcast.base_ref, f32[32,72,128]{2,1,0:T(8,128)} %copy-done.2), custom_call_target="tpu_custom_call" | custom-call | flops 4294967296 | bytes 2097152 | tf_op jit(solution)/shard_map/light/pallas_call | solution.py:378
  52.1 0.6 %copy.8 = f32[128,128]{1,0:T(8,128)} copy(f32[128,128]{1,0:T(8,128)S(1)} %get-tuple-element.9) | data formatting | bytes 131072
Async XLA Ops:
  0.6 3.4 %copy-start.3 = (s32[2048]{0:T(1024)S(1)}, s32[2048]{0:T(1024)}, u32[]{:S(2)}) copy-start(s32[2048]{0:T(1024)} %param.7) | copy-start | bytes 24580
  0.6 3.7 %copy-start.1 = (s32[8192]{0:T(1024)S(1)}, s32[8192]{0:T(1024)}, u32[]{:S(2)}) copy-start(s32[8192]{0:T(1024)} %param.6) | copy-start | bytes 98308
  4.4 1.1 %copy-start = (f32[16,72,128]{2,1,0:T(8,128)S(1)}, f32[16,72,128]{2,1,0:T(8,128)}, u32[]{:S(2)}) copy-start(f32[16,72,128]{2,1,0:T(8,128)} %pack.1.payload) | copy-start | bytes 1769476
  43.1 1.0 %copy-start.2 = (f32[32,72,128]{2,1,0:T(8,128)}, f32[32,72,128]{2,1,0:T(8,128)S(1)}, u32[]{:S(2)}) copy-start(f32[32,72,128]{2,1,0:T(8,128)S(1)} %get-tuple-element.4.got) | copy-start | bytes 3538948
